TPU v7x, 32 devices: a whole 2x2x4 slice. The times are simulated.
32 devices in a mesh: kv: 16 (over z, x, core), tp: 2 (over y).
Axes of the slice: x: 2, y: 2, z: 4, core: 2. Of those that a mesh axis runs over, the one named last changes fastest.
Arguments:
- queries: bfloat16 [16, 128, 576], P(None, 'tp'), may hold values from -36 to 36
- cache: bfloat16 [16, 4096, 576], P(None, 'kv'), may hold values from -6 to 6
- lengths: int32 [16], replicated, may hold values from 1 to 4096, as said below
- w_ov: bfloat16 [128, 512, 7168], P('tp', None, 'kv'), may hold values from -0.0234375 to 0.0234375
- resid: bfloat16 [16, 7168], P(None, 'tp'), may hold values from -3 to 3
- gain: float32 [7168], P('tp'), may hold values from 0.5 to 1.5
- w_gate: bfloat16 [7168, 18432], P('tp', 'kv'), may hold values from -0.0625 to 0.0625
- w_up: bfloat16 [7168, 18432], P('tp', 'kv'), may hold values from -0.0625 to 0.0625
- w_down: bfloat16 [18432, 7168], P('kv', 'tp'), may hold values from -0.046875 to 0.046875
Outputs:
- layer_out: bfloat16 [16, 7168], P(None, 'tp')
Inputs may be any that keep to these rules, and one draw needn't show every extreme that they name: Sequence b attends to positions 0 to lengths[b] - 1; in every draw some sequence has all 4096 positions live.
All inputs are finite; a program needn't handle non-finite values.
Results may differ from a plain program's by a relative error of at most 0.006.
Values sent between devices are 32-bit elements; how exact they have to be, the bound alone decides.
A program may use at most 128 MiB of HBM per device.

v0:
```python
import jax
import jax.numpy as jnp
from jax import lax
from jax.sharding import PartitionSpec as P

D = 7168
LAT = 512


softmax_scale = 192.0 ** (-0.5)
masked_score = -1e30
norm_floor = 0.05


def per_device(queries, cache, lengths, w_ov, resid, gain, w_gate, w_up, w_down):
    rows = cache.shape[1]
    first_row = lax.axis_index("kv") * rows
    place = first_row + lax.iota(jnp.int32, rows)
    live = (place[None, :] < lengths[:, None])[:, None, :]
    scores = (
        jnp.einsum("bhc,brc->bhr", queries, cache, preferred_element_type=jnp.float32)
        * softmax_scale
    )
    scores = jnp.where(live, scores, masked_score)
    peak = jnp.max(scores, axis=2)
    weights = jnp.where(live, jnp.exp(scores - peak[:, :, None]), 0.0)
    total = jnp.sum(weights, axis=2)
    mixed = jnp.einsum(
        "bhr,brc->bhc",
        weights.astype(jnp.bfloat16),
        cache[:, :, :LAT],
        preferred_element_type=jnp.float32,
    )
    top = lax.pmax(peak, "kv")
    factor = jnp.exp(peak - top)
    total, mixed = lax.psum((total * factor, mixed * factor[:, :, None]), "kv")
    heads_out = mixed / total[:, :, None]
    attn_part = jnp.einsum(
        "bhc,hcd->bd", heads_out.astype(jnp.bfloat16), w_ov, preferred_element_type=jnp.float32
    )
    partial_rows = lax.all_gather(attn_part, "kv", axis=1, tiled=True)
    attn = lax.psum_scatter(partial_rows, "tp", scatter_dimension=1, tiled=True)
    state = resid.astype(jnp.float32) + attn
    squares = lax.psum(jnp.sum(state * state, axis=1), "tp")
    scaled = (state * lax.rsqrt(squares / D + norm_floor)[:, None] * gain[None, :]).astype(
        jnp.bfloat16
    )
    gate_part = jnp.dot(scaled, w_gate, preferred_element_type=jnp.float32)
    up_part = jnp.dot(scaled, w_up, preferred_element_type=jnp.float32)
    gate, up = lax.psum((gate_part, up_part), "tp")
    inner = (jax.nn.silu(gate) * up).astype(jnp.bfloat16)
    ffn = lax.psum(jnp.dot(inner, w_down, preferred_element_type=jnp.float32), "kv")
    return (state + ffn).astype(jnp.bfloat16)


def solution(mesh):
    in_specs = (
        P(None, "tp", None),
        P(None, "kv", None),
        P(),
        P("tp", None, "kv"),
        P(None, "tp"),
        P("tp"),
        P("tp", "kv"),
        P("tp", "kv"),
        P("kv", "tp"),
    )
    out_specs = P(None, "tp")
    return jax.shard_map(
        per_device, mesh=mesh, in_specs=in_specs, out_specs=out_specs, check_vma=False
    )
```

profile of v0, /device:TPU:8, one launch (start us, length us, event | category | flops | bytes accessed | tf_op | source)
XLA Modules:
  0.0 339.4 jit_solution(5535327075866248540)
XLA Ops:
  6.5 0.8 broadcast_compare_fusion
  7.4 0.5 copy-done
  7.9 3.4 fusion.18
  11.3 25.9 %pmax.7 = f32[16,64]{1,0:T(8,128)S(1)} all-reduce(f32[16,64]{1,0:T(8,128)S(1)} %get-tuple-element.9), channel_id=1, replica_groups=mesh['kv'=16,'tp'=2] {'kv'}, use_global_device_ids=true, to_apply=%region_1.2 | all-reduce | flops 1024 | bytes 8192 | tf_op jit(solution)/shard_map/pmax | solution.py:34
  37.2 0.4 fusion.7
  37.6 4.9 %fusion.2 = f32[16,64,512]{2,1,0:T(8,128)} fusion(bf16[16,256,576]{1,2,0:T(8,128)(2,1)} %param.10, f32[16,64]{1,0:T(8,128)S(1)} %get-tuple-element.8, f32[16,64,256]{2,1,0:T(8,128)S(1)} %get-tuple-element.10, f32[16,64]{1,0:T(8,128)S(1)} %get-tuple-element.9, pred[16,256]{1,0:T(8,128)(4,1)S(1)} %broadcast_compare_fusion), kind=kOutput, calls=%fused_computation.3 | convolution fusion | flops 269746176 | bytes 7352320 | tf_op jit(solution)/shard_map/bhr,brc->bhc/dot_general | solution.py:28
  42.5 0.0 all-reduce.5.cloned.1.call-update
  42.5 0.0 reduce-scatter.2.cloned.1.call-start
  42.6 30.3 %psum.43 = f32[16,64]{1,0:T(8,128)S(1)} all-reduce(f32[16,64]{1,0:T(8,128)S(1)} %get-tuple-element.7), channel_id=1, replica_groups=mesh['kv'=16,'tp'=2] {'kv'}, use_global_device_ids=true, to_apply=%region_4.5 | all-reduce | flops 1024 | bytes 8192 | tf_op jit(solution)/shard_map/psum | solution.py:36
  72.8 73.7 %all-reduce.5.cloned.1.call-done = f32[16,64,512]{2,1,0:T(8,128)} async-done(((f32[16,64,512]{2,1,0:T(8,128)}), f32[16,64,512]{2,1,0:T(8,128)}) %all-reduce.5.cloned.1.call-update) | async-done | bytes 2097168 | tf_op jit(solution)/shard_map/psum | solution.py:36
  146.5 1.8 divide_convert_fusion
  148.3 0.0 copy-start.3
  148.3 0.0 copy-start.4
  148.3 13.3 %convolution_bitcast_fusion = f32[1,448,16]{1,2,0:T(8,128)S(1)} fusion(bf16[64,512,448]{1,2,0:T(8,128)(2,1)} %param.12, bf16[16,64,512]{2,1,0:T(8,128)(2,1)S(1)} %divide_convert_fusion), kind=kOutput, calls=%fused_computation.6 | convolution fusion | flops 469762048 | bytes 30437376 | tf_op jit(solution)/shard_map/bhc,hcd->bd/dot_general | solution.py:38
  161.6 18.3 %all-gather = f32[16,448,16]{1,2,0:T(8,128)S(1)} all-gather(f32[1,448,16]{1,2,0:T(8,128)S(1)} %convolution_bitcast_fusion), channel_id=1, replica_groups=mesh['kv'=16,'tp'=2] {'kv'}, dimensions={0}, use_global_device_ids=true | all-gather | bytes 487424 | tf_op jit(solution)/shard_map/all_gather | solution.py:41
  179.9 0.3 copy.17
  180.2 1.0 reshape.33
  181.2 0.0 reduce-scatter.2.cloned.1.call-update
  181.2 0.0 all-reduce.9.cloned.1.call-start
  181.3 14.0 %reduce-scatter.2.cloned.1.call-done = f32[16,3584]{1,0:T(8,128)} async-done(((f32[16,7168]{1,0:T(8,128)}), f32[16,3584]{1,0:T(8,128)}) %reduce-scatter.2.cloned.1.call-update) | async-done | bytes 229392 | tf_op jit(solution)/shard_map/reduce_scatter | solution.py:42
  195.3 1.1 multiply_reduce_fusion
  196.3 4.9 %psum.44 = f32[16]{0:T(128)S(1)} all-reduce(f32[16]{0:T(128)S(1)} %multiply_reduce_fusion), channel_id=1, replica_groups=mesh['kv'=16,'tp'=2] {'tp'}, use_global_device_ids=true, to_apply=%region_7.8 | all-reduce | flops 16 | bytes 128 | tf_op jit(solution)/shard_map/psum | solution.py:44
  201.3 1.0 multiply_convert_fusion
  202.3 5.2 %fusion.20 = f32[16,1152]{1,0:T(8,128)} fusion(bf16[16,3584]{1,0:T(8,128)(2,1)S(1)} %multiply_convert_fusion, bf16[3584,1152]{1,0:T(8,128)(2,1)} %param.16), kind=kOutput, calls=%fused_computation.30 | convolution fusion | flops 132120576 | bytes 8445952 | tf_op jit(solution)/shard_map/dot_general | solution.py:49
  207.5 5.1 %fusion.19 = f32[16,1152]{1,0:T(8,128)} fusion(bf16[16,3584]{1,0:T(8,128)(2,1)S(1)} %multiply_convert_fusion, bf16[3584,1152]{1,0:T(8,128)(2,1)} %param.15), kind=kOutput, calls=%fused_computation.29 | convolution fusion | flops 132120576 | bytes 8445952 | tf_op jit(solution)/shard_map/dot_general | solution.py:48
  212.6 0.0 all-reduce.9.cloned.1.call-update
  212.6 0.0 all-reduce.7.cloned.1.call-start
  212.7 21.9 %all-reduce.9.cloned.1.call-done = (f32[16,1152]{1,0:T(8,128)}, f32[16,1152]{1,0:T(8,128)}) async-done(((f32[16,1152]{1,0:T(8,128)}, f32[16,1152]{1,0:T(8,128)}), (f32[16,1152]{1,0:T(8,128)}, f32[16,1152]{1,0:T(8,128)})) %all-reduce.9.cloned.1.call-update) | async-done | bytes 147472 | tf_op jit(solution)/shard_map/psum | solution.py:50
  234.6 5.4 %fusion.13 = f32[16,3584]{1,0:T(8,128)} fusion(bf16[1152,3584]{1,0:T(8,128)(2,1)} %param.17, f32[16,1152]{1,0:T(8,128)} %get-tuple-element.5, f32[16,1152]{1,0:T(8,128)} %get-tuple-element.6), kind=kOutput, calls=%fused_computation.19 | convolution fusion | flops 132231168 | bytes 8634368 | tf_op jit(solution)/shard_map/dot_general | solution.py:52
  240.0 0.0 all-reduce.7.cloned.1.call-update
  240.0 91.2 %all-reduce.7.cloned.1.call-done = f32[16,3584]{1,0:T(8,128)} async-done(((f32[16,3584]{1,0:T(8,128)}), f32[16,3584]{1,0:T(8,128)}) %all-reduce.7.cloned.1.call-update) | async-done | bytes 229392 | tf_op jit(solution)/shard_map/psum | solution.py:52
  331.3 1.6 add_convert_fusion
  (11 shorter events, 0.0 us)
Async XLA Ops:
  6.5 1.3 copy-start
  6.5 140.0 %all-reduce.5.cloned.1.call-start = ((), (), s32[]{:S(2)}) async-start(), calls=%async_computation.1 | async-start | bytes 4194304 | tf_op jit(solution)/shard_map/psum | solution.py:36
  42.5 152.7 %reduce-scatter.2.cloned.1.call-start = ((), (), s32[]{:S(2)}) async-start(), calls=%async_computation.2 | async-start | bytes 688128 | tf_op jit(solution)/shard_map/reduce_scatter | solution.py:42
  148.3 46.9 %copy-start.3 = (bf16[16,3584]{1,0:T(8,128)(2,1)S(1)}, bf16[16,3584]{1,0:T(8,128)(2,1)}, u32[]{:S(2)}) copy-start(bf16[16,3584]{1,0:T(8,128)(2,1)} %param.13) | copy-start | bytes 344068
  148.3 53.0 %copy-start.4 = (f32[3584]{0:T(1024)S(1)}, f32[3584]{0:T(1024)}, u32[]{:S(2)}) copy-start(f32[3584]{0:T(1024)} %param.14) | copy-start | bytes 43012
  181.2 53.3 %all-reduce.9.cloned.1.call-start = ((), (), s32[]{:S(2)}) async-start(), calls=%async_computation.4 | async-start | bytes 294912 | tf_op jit(solution)/shard_map/psum | solution.py:50
  212.6 118.6 %all-reduce.7.cloned.1.call-start = ((), (), s32[]{:S(2)}) async-start(), calls=%async_computation.3 | async-start | bytes 458752 | tf_op jit(solution)/shard_map/psum | solution.py:52
  234.6 98.3 %copy-start.1 = (bf16[16,64,576]{2,1,0:T(8,128)(2,1)S(1)}, bf16[16,64,576]{2,1,0:T(8,128)(2,1)}, u32[]{:S(2)}) copy-start(bf16[16,64,576]{2,1,0:T(8,128)(2,1)} %param.9) | copy-start | bytes 3538948
  234.6 96.7 %copy-start.2 = (f32[16,3584]{1,0:T(8,128)S(1)}, f32[16,3584]{1,0:T(8,128)}, u32[]{:S(2)}) copy-start(f32[16,3584]{1,0:T(8,128)} %reduce-scatter.2.cloned.1.call-done) | copy-start | bytes 688132
Sparse Core Ops, SparseCore 0:
  42.6 103.8 all-reduce.4
  181.4 13.8 reduce-scatter.1
  212.8 21.7 all-reduce.8
  240.1 91.0 all-reduce.6
where the time goes:
time: 340 us; the launch traced here: 339 us
  waiting for transfers between devices  201 us (59%)
  blocking collectives  79.4 us (23%)
  matrix products  37.3 us (11%)
  between operations  13.2 us (4%)
  other arithmetic  6.8 us (2%)
    psum x1, waiting for transfers between devices, per_device(): lax.psum(jnp.dot(inner, w_down, preferred_element_type=jnp.float32), 'kv')  91.2 us
    psum x1, waiting for transfers between devices, per_device(): total, mixed = lax.psum((total * factor, mixed * factor[:, :, None]), 'kv')  73.7 us
    psum x1, blocking collectives, per_device(): total, mixed = lax.psum((total * factor, mixed * factor[:, :, None]), 'kv')  30.3 us
    pmax x1, blocking collectives, per_device(): top = lax.pmax(peak, 'kv')  25.9 us
    psum x1, waiting for transfers between devices, per_device(): gate, up = lax.psum((gate_part, up_part), 'tp')  21.9 us
    all_gather x1, blocking collectives, per_device(): partial_rows = lax.all_gather(attn_part, 'kv', axis=1, tiled=True)  18.3 us
    reduce_scatter x1, waiting for transfers between devices, per_device(): attn = lax.psum_scatter(partial_rows, 'tp', scatter_dimension=1, tiled=True)  14 us
    dot_general x1, matrix products, per_device(): jnp.einsum('bhc,hcd->bd', heads_out.astype(jnp.bfloat16), w_ov, preferred...  13.3 us
  transfers between devices with their start and end apart: 4, of which 4 were waited for; matrix products, arithmetic and copies ran while one was open for 0% of the time, Pallas kernels for 0%

commit v1 on v0

v1 whole, which is shorter than its diff:
```python
import functools

import jax
import jax.numpy as jnp
from jax import lax
from jax.experimental import pallas as pl
from jax.experimental.pallas import tpu as pltpu
from jax.sharding import PartitionSpec as P

LAT = 512
MESH = pl.DeviceIdType.MESH
F32 = jnp.float32
BF16 = jnp.bfloat16

softmax_scale = 192.0 ** (-0.5)
masked_score = -1e30
norm_floor = 0.05


def layer_kernel(
    n, nt, chunks, width_all,
    stats, mixed, resid, gain, wov_hbm, wg_hbm, wu_hbm, wd_hbm,
    out,
    sx, buf, r1, r2, r3, fin, wov, wg, wu, wd, pa, pr, pb, gath, st, sg, gu, gur, sqb, sqr,
    fp, f1, fa, f2, fb, f3, fin2,
    wsem, sx_s, sx_r, c_s, c_r, z_s, z_r, t_s, t_r, b_s, b_r, f_s, f_r, fz_s, fz_r,
):
    heads, batch, lat = mixed.shape
    nz = n // 4
    hc = heads // chunks
    half, quarter = hc // 2, hc // 4
    rows = quarter * batch // nz
    slots = wov.shape[0]
    me, tp = lax.axis_index("kv"), lax.axis_index("tp")
    c, x, z = lax.rem(me, 2), lax.rem(me // 2, 2), me // 4
    core_peer, x_peer = me + 1 - 2 * c, me + 2 - 4 * x

    def z_peer(d):
        return lax.rem(z + d, nz) * 4 + x * 2 + c

    def send(src, dst, s, r, **where):
        copy = pltpu.make_async_remote_copy(
            src_ref=src, dst_ref=dst, send_sem=s, recv_sem=r, device_id=where, device_id_type=MESH
        )
        copy.start()
        return copy

    loads = {}

    def load_ov(ch):
        loads[ch] = pltpu.make_async_copy(
            wov_hbm.at[pl.ds(ch * hc, hc)], wov.at[ch % slots], wsem.at[ch]
        )
        loads[ch].start()

    for ch in range(slots):
        load_ov(ch)
    others = []
    for i, (a, b) in enumerate(((wg_hbm, wg), (wu_hbm, wu), (wd_hbm, wd))):
        copy = pltpu.make_async_copy(a, b, wsem.at[chunks + i])
        copy.start()
        others.append(copy)

    barrier = pltpu.get_barrier_semaphore()
    for d in range(1, n):
        pl.semaphore_signal(barrier, inc=1, device_id={"kv": lax.rem(me + d, n)}, device_id_type=MESH)
    for d in range(1, nt):
        pl.semaphore_signal(barrier, inc=1, device_id={"tp": lax.rem(tp + d, nt)}, device_id_type=MESH)
    pl.semaphore_wait(barrier, n - 1 + nt - 1)

    copies = [
        send(stats, sx.at[d - 1], sx_s.at[d - 1], sx_r.at[d - 1], kv=lax.rem(me + d, n))
        for d in range(1, n)
    ]
    for copy in copies:
        copy.wait()
    peak, total = stats[0], stats[1]
    top = peak
    for d in range(n - 1):
        top = jnp.maximum(top, sx[d, 0])
    factor = jnp.exp(peak - top)
    whole = total * factor
    for d in range(n - 1):
        whole = whole + sx[d, 1] * jnp.exp(sx[d, 0] - top)
    factor = factor / whole

    def piece(ref, h0, zz):
        if rows % batch == 0:
            return ref.at[pl.ds(h0 + zz * (rows // batch), rows // batch)]
        return ref.at[h0 + zz * rows // batch, pl.ds(pl.multiple_of(lax.rem(zz * rows, batch), rows), rows)]

    flight = {}
    acc = [jnp.zeros((batch, pa.shape[1]), F32)]

    def stage(ch, s):
        b = ch * hc
        h0 = b + c * half
        q0 = h0 + x * quarter
        for copy in flight.pop(ch, ()):
            copy.wait()
        if s == 0:
            for i in range(hc):
                buf[b + i] = mixed[b + i] * factor[:, b + i : b + i + 1]
            flight[ch] = [
                send(buf.at[pl.ds(b + (1 - c) * half, half)], r1.at[ch], c_s.at[ch, 0], c_r.at[ch, 0], kv=core_peer)
            ]
        elif s == 1:
            for i in range(half):
                buf[h0 + i] = buf[h0 + i] + r1[ch, i]
            flight[ch] = [
                send(buf.at[pl.ds(h0 + (1 - x) * quarter, quarter)], r2.at[ch], c_s.at[ch, 1], c_r.at[ch, 1], kv=x_peer)
            ]
        elif s == 2:
            for i in range(quarter):
                buf[q0 + i] = buf[q0 + i] + r2[ch, i]
            flight[ch] = [
                send(piece(buf, q0, lax.rem(z + d, nz)), r3.at[ch, d - 1], z_s.at[ch, 0, d - 1], z_r.at[ch, 0, d - 1], kv=z_peer(d))
                for d in range(1, nz)
            ]
        elif s == 3:
            own = piece(buf, q0, z)[...]
            for d in range(nz - 1):
                own = own + r3[ch, d].reshape(own.shape)
            mine = piece(fin, q0, z)
            mine[...] = own
            flight[ch] = [
                send(mine, mine, z_s.at[ch, 1, d - 1], z_r.at[ch, 1, d - 1], kv=z_peer(d)) for d in range(1, nz)
            ]
        elif s == 4:
            part = fin.at[pl.ds(q0, quarter)]
            flight[ch] = [send(part, part, c_s.at[ch, 2], c_r.at[ch, 2], kv=x_peer)]
        elif s == 5:
            part = fin.at[pl.ds(h0, half)]
            flight[ch] = [send(part, part, c_s.at[ch, 3], c_r.at[ch, 3], kv=core_peer)]
        else:
            loads[ch].wait()

            def body(i, a):
                return a + jnp.dot(fin[b + i].astype(BF16), wov[ch % slots, i], preferred_element_type=F32)

            acc[0] = lax.fori_loop(0, hc, body, acc[0])
            if ch + slots < chunks:
                load_ov(ch + slots)

    for t in range(chunks + 6):
        turn = [(ch, t - ch) for ch in range(chunks) if 0 <= t - ch <= 6]
        for ch, s in sorted(turn, key=lambda e: e[1] == 6):
            stage(ch, s)

    pa[...] = acc[0]
    copies = [
        send(pa, pr.at[d - 1], t_s.at[0, d - 1], t_r.at[0, d - 1], tp=lax.rem(tp + d, nt)) for d in range(1, nt)
    ]
    own = pa[...]
    for copy in copies:
        copy.wait()
    for d in range(nt - 1):
        own = own + pr[d]
    pb[...] = own
    per = n // nt
    slot = lax.rem(me, per)
    owner = me // per == tp

    def spread(d):
        return pltpu.make_async_remote_copy(
            src_ref=pb, dst_ref=gath.at[slot], send_sem=b_s.at[d - 1], recv_sem=b_r.at[slot],
            device_id={"kv": lax.rem(me + d, n)}, device_id_type=MESH,
        )

    @pl.when(owner)
    def _():
        for d in range(1, n):
            spread(d).start()
        gath[slot] = pb[...]
        for d in range(1, n):
            spread(d).wait_send()

    for j in range(per):
        @pl.when(tp * per + j != me)
        def _():
            pltpu.make_async_remote_copy(
                src_ref=pb, dst_ref=gath.at[j], send_sem=b_s.at[0], recv_sem=b_r.at[j],
                device_id={"kv": me}, device_id_type=MESH,
            ).wait_recv()

    cols = pb.shape[1]
    for j in range(per):
        st[:, j * cols : (j + 1) * cols] = gath[j]
    state = st[...] + resid[...].astype(F32)
    st[...] = state
    sqb[...] = jnp.broadcast_to(jnp.sum(state * state, axis=1, keepdims=True), sqb.shape)
    sg[...] = (state * gain[...]).astype(BF16)

    width, hidden = wg.shape
    step = 512 if width % 512 == 0 else 128
    others[0].wait()
    others[1].wait()

    def project(i, carry):
        ga, ua = carry
        k = pl.ds(pl.multiple_of(i * step, step), step)
        left = sg[:, k]
        return (
            ga + jnp.dot(left, wg[k, :], preferred_element_type=F32),
            ua + jnp.dot(left, wu[k, :], preferred_element_type=F32),
        )

    zero = jnp.zeros((batch, hidden), F32)
    ga, ua = lax.fori_loop(0, width // step, project, (zero, zero))
    gu[0] = ga
    gu[1] = ua
    copies = []
    for d in range(1, nt):
        peer = lax.rem(tp + d, nt)
        copies.append(send(gu, gur.at[d - 1], t_s.at[1, d - 1], t_r.at[1, d - 1], tp=peer))
        copies.append(send(sqb, sqr.at[d - 1], t_s.at[2, d - 1], t_r.at[2, d - 1], tp=peer))
    for copy in copies:
        copy.wait()
    gate, up, squares = gu[0], gu[1], sqb[...]
    for d in range(nt - 1):
        gate, up, squares = gate + gur[d, 0], up + gur[d, 1], squares + sqr[d]
    inv = lax.rsqrt(squares[:, :1] / width_all + norm_floor)
    gate, up = gate * inv, up * inv
    inner = (gate / (1.0 + jnp.exp(-gate)) * up).astype(BF16)

    others[2].wait()
    wh = width // 2
    if wh % 256 == 0:
        for i in range(2):
            for k in range(0, wh, 256):
                fp[i, :, k : k + 256] = jnp.dot(
                    inner, wd[:, i * wh + k : i * wh + k + 256], preferred_element_type=F32
                )
    else:
        y = jnp.dot(inner, wd[...], preferred_element_type=F32)
        fp[0] = y[:, :wh]
        fp[1] = y[:, wh:]

    hb = batch // 2
    mine = pl.ds(pl.multiple_of(c * hb, hb), hb)
    theirs = pl.ds(pl.multiple_of((1 - c) * hb, hb), hb)
    send(fp.at[:, theirs, :], f1, f_s.at[0], f_r.at[0], kv=core_peer).wait()
    fa[...] = fp[:, mine, :] + f1[...]
    send(fa.at[1 - x], f2, f_s.at[1], f_r.at[1], kv=x_peer).wait()
    summed = fa[x] + f2[...]
    fb[...] = summed
    f3[z] = summed
    copies = [
        send(fb, f3.at[z], fz_s.at[d - 1], fz_r.at[d - 1], kv=z_peer(d)) for d in range(1, nz)
    ]
    for copy in copies:
        copy.wait()
    summed = f3[0]
    for i in range(1, nz):
        summed = summed + f3[i]
    fin2[x, mine, :] = summed
    part = fin2.at[x, mine, :]
    send(part, part, f_s.at[2], f_r.at[2], kv=x_peer).wait()
    part = fin2.at[:, mine, :]
    send(part, part, f_s.at[3], f_r.at[3], kv=core_peer).wait()
    for i in range(2):
        out[:, i * wh : (i + 1) * wh] = (st[:, i * wh : (i + 1) * wh] + fin2[i]).astype(out.dtype)


def per_device(n, nt, queries, cache, lengths, w_ov, resid, gain, w_gate, w_up, w_down):
    rows = cache.shape[1]
    first_row = lax.axis_index("kv") * rows
    place = first_row + lax.iota(jnp.int32, rows)
    live = (place[None, :] < lengths[:, None])[:, None, :]
    scores = jnp.einsum("bhc,brc->bhr", queries, cache, preferred_element_type=F32) * softmax_scale
    scores = jnp.where(live, scores, masked_score)
    peak = jnp.max(scores, axis=2)
    weights = jnp.where(live, jnp.exp(scores - peak[:, :, None]), 0.0)
    total = jnp.sum(weights, axis=2)
    mixed = jnp.einsum(
        "bhr,brc->hbc", weights.astype(BF16), cache[:, :, :LAT], preferred_element_type=F32
    )
    stats = jnp.stack([peak, total])

    batch, heads = peak.shape
    chunks = max(1, heads // 16)
    hc = heads // chunks
    nz = n // 4
    quarter = hc // 4
    piece_rows = quarter * batch // nz
    lat = LAT
    cols = w_ov.shape[2]
    width, hidden = w_gate.shape
    wh, hb = width // 2, batch // 2
    slots = min(3, chunks)
    if piece_rows % batch == 0:
        r3 = (chunks, nz - 1, piece_rows // batch, batch, lat)
    else:
        r3 = (chunks, nz - 1, piece_rows, lat)
    vm = pltpu.VMEM
    dma = pltpu.SemaphoreType.DMA
    scratch = [
        vm((n - 1, 2, batch, heads), F32),
        vm((heads, batch, lat), F32),
        vm((chunks, hc // 2, batch, lat), F32),
        vm((chunks, quarter, batch, lat), F32),
        vm(r3, F32),
        vm((heads, batch, lat), F32),
        vm((slots, hc, lat, cols), BF16),
        vm((width, hidden), BF16),
        vm((width, hidden), BF16),
        vm((hidden, width), BF16),
        vm((batch, cols), F32),
        vm((nt - 1, batch, cols), F32),
        vm((batch, cols), F32),
        vm((n // nt, batch, cols), F32),
        vm((batch, width), F32),
        vm((batch, width), BF16),
        vm((2, batch, hidden), F32),
        vm((nt - 1, 2, batch, hidden), F32),
        vm((batch, 128), F32),
        vm((nt - 1, batch, 128), F32),
        vm((2, batch, wh), F32),
        vm((2, hb, wh), F32),
        vm((2, hb, wh), F32),
        vm((hb, wh), F32),
        vm((hb, wh), F32),
        vm((nz, hb, wh), F32),
        vm((2, batch, wh), F32),
        dma((chunks + 3,)),
        dma((n - 1,)), dma((n - 1,)),
        dma((chunks, 4)), dma((chunks, 4)),
        dma((chunks, 2, nz - 1)), dma((chunks, 2, nz - 1)),
        dma((3, nt - 1)), dma((3, nt - 1)),
        dma((n - 1,)), dma((n // nt,)),
        dma((4,)), dma((4,)),
        dma((nz - 1,)), dma((nz - 1,)),
    ]
    in_vmem = pl.BlockSpec(memory_space=pltpu.VMEM)
    in_hbm = pl.BlockSpec(memory_space=pl.ANY)
    return pl.pallas_call(
        functools.partial(layer_kernel, n, nt, chunks, width * nt),
        out_shape=jax.ShapeDtypeStruct((batch, width), BF16),
        in_specs=[in_vmem] * 4 + [in_hbm] * 4,
        out_specs=in_vmem,
        scratch_shapes=scratch,
        compiler_params=pltpu.CompilerParams(
            collective_id=0, has_side_effects=True, vmem_limit_bytes=63 * 1024 * 1024
        ),
    )(stats, mixed, resid, gain.reshape(1, width), w_ov, w_gate, w_up, w_down)


def solution(mesh):
    in_specs = (
        P(None, "tp", None),
        P(None, "kv", None),
        P(),
        P("tp", None, "kv"),
        P(None, "tp"),
        P("tp"),
        P("tp", "kv"),
        P("tp", "kv"),
        P("kv", "tp"),
    )
    return jax.shard_map(
        functools.partial(per_device, mesh.shape["kv"], mesh.shape["tp"]),
        mesh=mesh,
        in_specs=in_specs,
        out_specs=P(None, "tp"),
        check_vma=False,
    )
```

time: 340 us -> 152 us (0.45)
  waiting for transfers between devices: 201 us -> 0 us
  Pallas kernels: 0 us -> 97.3 us
  blocking collectives: 79.4 us -> 0 us
  local copies, waits for them, and re-layouts: 1.81 us -> 44.7 us
  matrix products: 37.3 us -> 5.33 us
  between operations: 13.2 us -> 0.03 us
  other arithmetic: 6.8 us -> 1.91 us
    psum x3 -> x0, waiting for transfers between devices: 187 us -> none  [the longest x1 91.2 us: per_device(): lax.psum(jnp.dot(inner, w_down, preferred_element_type=jnp.float32), 'kv')]
    pallas_call x0 -> x1, Pallas kernels: none -> 97.3 us  [per_device(): pl.pallas_call(functools.partial(layer_kernel, n, nt, chunks, width * nt)...]
    unnamed x11 -> x4, local copies, waits for them, and re-layouts: 1.5 us -> 40.6 us
    psum x2 -> x0, blocking collectives: 35.2 us -> none  [the longest x1 30.3 us: per_device(): total, mixed = lax.psum((total * factor, mixed * factor[:, :, None]), 'kv')]
    dot_general x6 -> x2, matrix products: 37.3 us -> 5.33 us  [the longest x1 3.8 us: per_device(): jnp.einsum('bhc,brc->bhr', queries, cache, preferred_element_type=F32)]
    pmax x1 -> x0, blocking collectives: 25.9 us -> none  [per_device(): top = lax.pmax(peak, 'kv')]
    all_gather x1 -> x0, blocking collectives: 18.3 us -> none  [per_device(): partial_rows = lax.all_gather(attn_part, 'kv', axis=1, tiled=True)]
    reduce_scatter x1 -> x0, waiting for transfers between devices: 14 us -> none  [per_device(): attn = lax.psum_scatter(partial_rows, 'tp', scatter_dimension=1, tiled=True)]
  transfers between devices with their start and end apart: 4 -> 0, of which waited for: 4 -> 0; matrix products, arithmetic and copies ran while one was open for 0% -> 0% of each run, Pallas kernels for 0% -> 0%
where the time goes in v1:
time: 152 us; the launch traced here: 149 us
  Pallas kernels  97.3 us (64%)
  local copies, waits for them, and re-layouts  44.7 us (29%)
  matrix products  5.33 us (4%)
  other arithmetic  1.91 us (1%)
    pallas_call x1, Pallas kernels, per_device(): pl.pallas_call(functools.partial(layer_kernel, n, nt, chunks, width * nt)...  97.3 us
    unnamed x4, local copies, waits for them, and re-layouts  40.6 us
    dot_general x1, matrix products, per_device(): jnp.einsum('bhc,brc->bhr', queries, cache, preferred_element_type=F32)  3.8 us

profile of v1, /device:TPU:8, one launch (start us, length us, event | category | flops | bytes accessed | tf_op | source)
XLA Modules:
  0.0 149.3 jit_solution(17792986778379217601)
XLA Ops:
  0.0 0.0 copy-start
  0.0 0.9 broadcast_compare_fusion
  0.9 1.5 %reshape.31.gain = f32[1,3584]{1,0:T(1,128)} reshape(f32[3584]{0:T(1024)} %param.14) | data formatting | bytes 28672 | tf_op jit(solution)/shard_map/reshape | solution.py:345
  2.4 3.8 %fusion.10 = (f32[16,64]{1,0:T(8,128)S(1)}, f32[16,64,256]{2,1,0:T(8,128)S(1)}) fusion(bf16[16,64,576]{2,1,0:T(8,128)(2,1)} %param.9, bf16[16,256,576]{1,2,0:T(8,128)(2,1)} %param.10, pred[16,256]{1,0:T(8,128)(4,1)S(1)} %broadcast_compare_fusion), kind=kOutput, calls=%fused_computation.15 | convolution fusion | flops 302775296 | bytes 6955008 | tf_op jit(solution)/shard_map/bhc,brc->bhr/dot_general | solution.py:270
  6.2 0.4 fusion.4
  6.6 0.6 pad_maximum_fusion.stats
  7.3 0.0 copy-done
  7.3 1.5 %fusion = f32[16,64,512]{2,1,0:T(8,128)S(1)} fusion(bf16[16,256,576]{1,2,0:T(8,128)(2,1)S(1)} %copy-done, f32[16,64,256]{2,1,0:T(8,128)S(1)} %get-tuple-element.6, f32[16,64]{1,0:T(8,128)S(1)} %get-tuple-element.5, pred[16,256]{1,0:T(8,128)(4,1)S(1)} %broadcast_compare_fusion), kind=kOutput, calls=%fused_computation | convolution fusion | flops 269221888 | bytes 7352320 | tf_op jit(solution)/shard_map/bhr,brc->hbc/dot_general | solution.py:275
  8.8 2.5 %copy.15 = f32[16,64,512]{2,0,1:T(8,128)} copy(f32[16,64,512]{2,1,0:T(8,128)S(1)} %fusion) | data formatting | bytes 4194304 | tf_op jit(solution)/shard_map/bhr,brc->hbc/dot_general | solution.py:275
  11.3 39.1 %copy.12.wov_hbm = bf16[64,512,448]{2,1,0:T(8,128)(2,1)} copy(bf16[64,512,448]{1,2,0:T(8,128)(2,1)} %param.12) | data formatting | bytes 58720256 | tf_op args[3]
  50.4 97.3 %shard_map.91 = bf16[16,3584]{1,0:T(8,128)(2,1)} custom-call(f32[2,16,64]{2,1,0:T(8,128)} %pad_maximum_fusion.stats, f32[64,16,512]{2,1,0:T(8,128)} %bitcast.7, bf16[16,3584]{1,0:T(8,128)(2,1)} %resid.1, f32[1,3584]{1,0:T(1,128)} %reshape.31.gain, bf16[64,512,448]{2,1,0:T(8,128)(2,1)} %copy.12.wov_hbm, bf16[3584,1152]{1,0:T(8,128)(2,1)} %wg_hbm.1, ...), custom_call_target="tpu_custom_call" | custom-call | tf_op jit(solution)/shard_map/pallas_call | solution.py:336
  147.7 1.6 %copy.17 = bf16[16,3584]{1,0:T(8,128)(2,1)} copy(bf16[16,3584]{1,0:T(8,128)(2,1)} %shard_map.91) | data formatting | bytes 229376
  (1 shorter events, 0.0 us)
Async XLA Ops:
  0.0 7.3 %copy-start = (bf16[16,256,576]{1,2,0:T(8,128)(2,1)S(1)}, bf16[16,256,576]{1,2,0:T(8,128)(2,1)}, u32[]{:S(2)}) copy-start(bf16[16,256,576]{1,2,0:T(8,128)(2,1)} %param.10) | copy-start | bytes 14155780

commit v2 on v1

--- a/solution.py
+++ b/solution.py
@@ -19,13 +19,15 @@
 
 def layer_kernel(
     n, nt, chunks, width_all,
-    stats, mixed, resid, gain, wov_hbm, wg_hbm, wu_hbm, wd_hbm,
+    lens, q_hbm, cache_hbm, resid, gain, wov_hbm, wg_hbm, wu_hbm, wd_hbm,
     out,
-    sx, buf, r1, r2, r3, fin, wov, wg, wu, wd, pa, pr, pb, gath, st, sg, gu, gur, sqb, sqr,
+    q, kt, wts, mixed, cols_ab, stats, qsem, ksem, sx, buf, r1, r2, r3, fin, wov, wg, wu, wd, pa, pr, pb, gath, st, sg, gu, gur, sqb, sqr,
     fp, f1, fa, f2, fb, f3, fin2,
     wsem, sx_s, sx_r, c_s, c_r, z_s, z_r, t_s, t_r, b_s, b_r, f_s, f_r, fz_s, fz_r,
 ):
-    heads, batch, lat = mixed.shape
+    batch, heads, _ = q.shape
+    lat = buf.shape[2]
+    rows_kv = kt.shape[2]
     nz = n // 4
     hc = heads // chunks
     half, quarter = hc // 2, hc // 4
@@ -45,6 +47,32 @@
         copy.start()
         return copy
 
+    fetch = [pltpu.make_async_copy(q_hbm, q, qsem)]
+    fetch += [pltpu.make_async_copy(cache_hbm.at[b], kt.at[b], ksem.at[b]) for b in range(batch)]
+    for copy in fetch:
+        copy.start()
+
+    barrier = pltpu.get_barrier_semaphore()
+    for d in range(1, n):
+        pl.semaphore_signal(barrier, inc=1, device_id={"kv": lax.rem(me + d, n)}, device_id_type=MESH)
+    for d in range(1, nt):
+        pl.semaphore_signal(barrier, inc=1, device_id={"tp": lax.rem(tp + d, nt)}, device_id_type=MESH)
+    place = me * rows_kv + lax.broadcasted_iota(jnp.int32, (heads, rows_kv), 1)
+    fetch[0].wait()
+    for b in range(batch):
+        fetch[1 + b].wait()
+        live = place < lens[b]
+        scores = jnp.dot(q[b], kt[b], preferred_element_type=F32) * softmax_scale
+        scores = jnp.where(live, scores, masked_score)
+        high = jnp.max(scores, axis=1, keepdims=True)
+        soft = jnp.where(live, jnp.exp(scores - high), 0.0)
+        wts[b] = soft.astype(BF16)
+        cols_ab[:, b : b + 1] = high
+        cols_ab[:, batch + b : batch + b + 1] = jnp.sum(soft, axis=1, keepdims=True)
+    turned = cols_ab[...].T
+    stats[0] = turned[:batch]
+    stats[1] = turned[batch : 2 * batch]
+
     loads = {}
 
     def load_ov(ch):
@@ -61,17 +89,18 @@
         copy.start()
         others.append(copy)
 
-    barrier = pltpu.get_barrier_semaphore()
-    for d in range(1, n):
-        pl.semaphore_signal(barrier, inc=1, device_id={"kv": lax.rem(me + d, n)}, device_id_type=MESH)
-    for d in range(1, nt):
-        pl.semaphore_signal(barrier, inc=1, device_id={"tp": lax.rem(tp + d, nt)}, device_id_type=MESH)
     pl.semaphore_wait(barrier, n - 1 + nt - 1)
 
     copies = [
         send(stats, sx.at[d - 1], sx_s.at[d - 1], sx_r.at[d - 1], kv=lax.rem(me + d, n))
         for d in range(1, n)
     ]
+    for b in range(batch):
+        whole_row = lax.dot_general(
+            wts[b], kt[b, :lat, :], (((1,), (1,)), ((), ())), preferred_element_type=F32
+        )
+        for k in range(lat // 128):
+            mixed[k, pl.ds(b * heads, heads), :] = whole_row[:, k * 128 : (k + 1) * 128]
     for copy in copies:
         copy.wait()
     peak, total = stats[0], stats[1]
@@ -100,7 +129,9 @@
             copy.wait()
         if s == 0:
             for i in range(hc):
-                buf[b + i] = mixed[b + i] * factor[:, b + i : b + i + 1]
+                scale = factor[:, b + i : b + i + 1]
+                for k in range(lat // 128):
+                    buf[b + i, :, k * 128 : (k + 1) * 128] = mixed[k, pl.ds(b + i, batch, stride=heads), :] * scale
             flight[ch] = [
                 send(buf.at[pl.ds(b + (1 - c) * half, half)], r1.at[ch], c_s.at[ch, 0], c_r.at[ch, 0], kv=core_peer)
             ]
@@ -136,7 +167,10 @@
             loads[ch].wait()
 
             def body(i, a):
-                return a + jnp.dot(fin[b + i].astype(BF16), wov[ch % slots, i], preferred_element_type=F32)
+                return a + lax.dot_general(
+                    fin[b + i].astype(BF16), wov[ch % slots, i], (((1,), (1,)), ((), ())),
+                    preferred_element_type=F32,
+                )
 
             acc[0] = lax.fori_loop(0, hc, body, acc[0])
             if ch + slots < chunks:
@@ -186,12 +220,12 @@
     cols = pb.shape[1]
     for j in range(per):
         st[:, j * cols : (j + 1) * cols] = gath[j]
+    width, hidden = wg.shape
     state = st[...] + resid[...].astype(F32)
     st[...] = state
     sqb[...] = jnp.broadcast_to(jnp.sum(state * state, axis=1, keepdims=True), sqb.shape)
-    sg[...] = (state * gain[...]).astype(BF16)
-
-    width, hidden = wg.shape
+    sg[...] = (state * gain[...].reshape(1, width)).astype(BF16)
+
     step = 512 if width % 512 == 0 else 128
     others[0].wait()
     others[1].wait()
@@ -263,21 +297,8 @@
 
 
 def per_device(n, nt, queries, cache, lengths, w_ov, resid, gain, w_gate, w_up, w_down):
-    rows = cache.shape[1]
-    first_row = lax.axis_index("kv") * rows
-    place = first_row + lax.iota(jnp.int32, rows)
-    live = (place[None, :] < lengths[:, None])[:, None, :]
-    scores = jnp.einsum("bhc,brc->bhr", queries, cache, preferred_element_type=F32) * softmax_scale
-    scores = jnp.where(live, scores, masked_score)
-    peak = jnp.max(scores, axis=2)
-    weights = jnp.where(live, jnp.exp(scores - peak[:, :, None]), 0.0)
-    total = jnp.sum(weights, axis=2)
-    mixed = jnp.einsum(
-        "bhr,brc->hbc", weights.astype(BF16), cache[:, :, :LAT], preferred_element_type=F32
-    )
-    stats = jnp.stack([peak, total])
-
-    batch, heads = peak.shape
+    batch, heads, entries = queries.shape
+    rows_kv = cache.shape[1]
     chunks = max(1, heads // 16)
     hc = heads // chunks
     nz = n // 4
@@ -295,13 +316,20 @@
     vm = pltpu.VMEM
     dma = pltpu.SemaphoreType.DMA
     scratch = [
+        vm((batch, heads, entries), BF16),
+        vm((batch, entries, rows_kv), BF16),
+        vm((batch, heads, rows_kv), BF16),
+        vm((lat // 128, batch * heads, 128), F32),
+        vm((heads, 128), F32),
+        vm((2, batch, heads), F32),
+        dma(()), dma((batch,)),
         vm((n - 1, 2, batch, heads), F32),
         vm((heads, batch, lat), F32),
         vm((chunks, hc // 2, batch, lat), F32),
         vm((chunks, quarter, batch, lat), F32),
         vm(r3, F32),
         vm((heads, batch, lat), F32),
-        vm((slots, hc, lat, cols), BF16),
+        vm((slots, hc, cols, lat), BF16),
         vm((width, hidden), BF16),
         vm((width, hidden), BF16),
         vm((hidden, width), BF16),
@@ -336,13 +364,13 @@
     return pl.pallas_call(
         functools.partial(layer_kernel, n, nt, chunks, width * nt),
         out_shape=jax.ShapeDtypeStruct((batch, width), BF16),
-        in_specs=[in_vmem] * 4 + [in_hbm] * 4,
+        in_specs=[pl.BlockSpec(memory_space=pltpu.SMEM)] + [in_hbm] * 2 + [in_vmem] * 2 + [in_hbm] * 4,
         out_specs=in_vmem,
         scratch_shapes=scratch,
         compiler_params=pltpu.CompilerParams(
             collective_id=0, has_side_effects=True, vmem_limit_bytes=63 * 1024 * 1024
         ),
-    )(stats, mixed, resid, gain.reshape(1, width), w_ov, w_gate, w_up, w_down)
+    )(lengths, queries, jnp.swapaxes(cache, 1, 2), resid, gain, jnp.swapaxes(w_ov, 1, 2), w_gate, w_up, w_down)
 
 
 def solution(mesh):

time: 152 us -> 108 us (0.71)
  local copies, waits for them, and re-layouts: 44.7 us -> 1.55 us
  Pallas kernels: 97.3 us -> 104 us
  matrix products: 5.33 us -> 0 us
  other arithmetic: 1.91 us -> 0 us
    unnamed x4 -> x1, local copies, waits for them, and re-layouts: 40.6 us -> 1.55 us
    pallas_call x1, Pallas kernels: 97.3 us -> 104 us  [per_device(): pl.pallas_call(functools.partial(layer_kernel, n, nt, chunks, width * nt)...]
    dot_general x2 -> x0, matrix products: 5.33 us -> none  [the longest x1 3.8 us: per_device(): jnp.einsum('bhc,brc->bhr', queries, cache, preferred_element_type=F32)]
    dot_general x1 -> x0, local copies, waits for them, and re-layouts: 2.53 us -> none  [per_device(): jnp.einsum('bhr,brc->hbc', weights.astype(BF16), cache[:, :, :LAT], prefe...]
    reshape x1 -> x0, local copies, waits for them, and re-layouts: 1.53 us -> none  [per_device(): gain.reshape(1, width)]
where the time goes in v2:
time: 108 us; the launch traced here: 106 us
  Pallas kernels  104 us (96%)
  local copies, waits for them, and re-layouts  1.55 us (1%)
    pallas_call x1, Pallas kernels, per_device(): pl.pallas_call(functools.partial(layer_kernel, n, nt, chunks, width * nt)...  104 us

profile of v2, /device:TPU:8, one launch (start us, length us, event | category | flops | bytes accessed | tf_op | source)
XLA Modules:
  0.0 105.6 jit_solution(4017367269527519199)
XLA Ops:
  0.0 104.0 %shard_map.91 = bf16[16,3584]{1,0:T(8,128)(2,1)} custom-call(s32[16]{0:T(128)} %lens.1, bf16[16,64,576]{2,1,0:T(8,128)(2,1)} %q_hbm.1, bf16[16,576,256]{2,1,0:T(8,128)(2,1)} %bitcast.3, bf16[16,3584]{1,0:T(8,128)(2,1)} %resid.1, f32[3584]{0:T(1024)} %gain.1, bf16[64,448,512]{2,1,0:T(8,128)(2,1)} %bitcast.2, bf16[3584,1152]{1,0:T(8,128)(2,1)} %wg_hbm.1, ...), custom_call_target="tpu_custom_call" | custom-call | tf_op jit(solution)/shard_map/pallas_call | solution.py:364
  104.0 1.6 %copy.11 = bf16[16,3584]{1,0:T(8,128)(2,1)} copy(bf16[16,3584]{1,0:T(8,128)(2,1)} %shard_map.91) | data formatting | bytes 229376
